TPU v7x, 256 devices: a whole 4x4x8 slice. The times are simulated.
256 devices in a mesh: dp: 8 (over z), expert: 32 (over x, y, core).
Axes of the slice: x: 4, y: 4, z: 8, core: 2. Of those that a mesh axis runs over, the one named last changes fastest.
Arguments:
- tokens: bfloat16 [65536, 2048], P(('dp', 'expert')), may hold values from -6 to 6
- expert_ranks: int32 [32, 65536], P(None, ('dp', 'expert')), may hold values from 0 to 65535, as said below
- capacity: int32 [32], replicated, may hold values from 512 to 1024, as said below
- weight_in: bfloat16 [32, 2048, 8192], P('expert', None, 'dp'), may hold values from -0.125 to 0.125
- weight_out: bfloat16 [32, 8192, 2048], P('expert', 'dp'), may hold values from -0.0625 to 0.0625
- gate_weights: float32 [32, 1024], P('expert', 'dp'), may hold values from 0.05 to 1
Outputs:
- combined: bfloat16 [65536, 2048], P(('dp', 'expert'))
Inputs may be any that keep to these rules, and one draw needn't show every extreme that they name: `expert_ranks`: for each expert the ranks are a permutation of 0 to 65535. Of the 256 tokens of one device, at most 8 have rank under 1024 for one expert; for an expert of capacity 1024, some devices have exactly 8. At least one expert has capacity 1024.
All inputs are finite; a program needn't handle non-finite values.
Results may differ from a plain program's by a relative error of at most 0.0053.
Values may be sent and summed in bfloat16 or wider, within the bound.
A program may use at most 64 MiB of HBM per device.

v0:
```python
import jax
import jax.numpy as jnp
from jax import lax
from jax.sharding import Mesh
from jax.sharding import PartitionSpec as P

MOST = 8
EXPERT = ("expert_0", "expert_1", "expert_2")
DP_EXPERT = ("dp", "expert_0", "expert_1", "expert_2")


def laid_out(blocks, dim):
    blocks = jnp.moveaxis(blocks, 0, dim)
    dims = blocks.shape
    return blocks.reshape(*dims[:dim], dims[dim] * dims[dim + 1], *dims[dim + 2 :])


def gather_in_order(array, axes, order):
    blocks = array[None]
    for k in order:
        blocks = lax.all_gather(blocks, axes[k], axis=0, tiled=True)
    block = [lax.axis_size(axes[k]) for k in reversed(order)]
    blocks = blocks.reshape(*block, *array.shape)
    turned = sorted(range(len(order)), key=lambda place: order[len(order) - 1 - place])
    return blocks.transpose(*turned, *range(len(order), blocks.ndim)).reshape(-1, *array.shape)


def gather_axes(array, axes, order, dim):
    return laid_out(gather_in_order(array, axes, order), dim)


def on_device(tokens, expert_ranks, capacity, weight_in, weight_out, gate_weights):
    dp_count = lax.axis_size("dp")
    expert_count = lax.axis_size(EXPERT)
    token_count, width = tokens.shape
    slots_all = gate_weights.shape[1] * dp_count
    chosen = expert_ranks < capacity[:, None]
    chosen_int = chosen.astype(jnp.int32)
    counts = jnp.sum(chosen_int, axis=1)
    before = jnp.cumsum(chosen_int, axis=1) - chosen_int
    places = lax.broadcasted_iota(jnp.int32, (expert_count, MOST, token_count), 1)
    pack_table = jnp.logical_and(chosen[:, None, :], before[:, None, :] == places)
    pack_table = pack_table.astype(jnp.bfloat16).reshape(expert_count * MOST, token_count)
    packed = jnp.dot(pack_table, tokens, preferred_element_type=jnp.float32).astype(jnp.bfloat16)
    arrived_rows = lax.all_to_all(
        packed.reshape(expert_count, MOST, width), EXPERT, split_axis=0, concat_axis=0, tiled=True
    )
    own_expert = lax.axis_index(EXPERT)
    expert_mask = (lax.broadcasted_iota(jnp.int32, (expert_count,), 0) == own_expert).astype(
        jnp.int32
    )
    count_table = gather_axes(counts[None, :], DP_EXPERT, (1, 0, 2, 3), 0)
    column = jnp.sum(count_table * expert_mask[None, :], axis=1)
    earlier_sums = jnp.cumsum(column) - column
    row_first = lax.axis_index("dp") * expert_count
    starts = lax.dynamic_slice_in_dim(earlier_sums, row_first, expert_count, 0)
    arrived = lax.dynamic_slice_in_dim(column, row_first, expert_count, 0)
    within = lax.broadcasted_iota(jnp.int32, (expert_count, MOST), 1)
    target = jnp.where(within < arrived[:, None], starts[:, None] + within, -1).reshape(
        expert_count * MOST
    )
    slot_ids = lax.broadcasted_iota(jnp.int32, (expert_count * MOST, slots_all), 1)
    place_table = (target[:, None] == slot_ids).astype(jnp.bfloat16)
    flat_rows = arrived_rows.reshape(expert_count * MOST, width)
    local_rows = lax.dot_general(
        place_table, flat_rows, (((0,), (0,)), ((), ())), preferred_element_type=jnp.float32
    ).astype(jnp.bfloat16)
    first_weight = weight_in[0]
    second_weight = weight_out[0]
    slot_rows = lax.psum(local_rows, "dp").astype(jnp.float32).astype(jnp.bfloat16)
    hidden = jnp.maximum(
        jnp.dot(slot_rows, first_weight, preferred_element_type=jnp.float32), 0.0
    ).astype(jnp.bfloat16)
    out_share = lax.psum_scatter(
        jnp.dot(hidden, second_weight, preferred_element_type=jnp.float32),
        "dp",
        scatter_dimension=0,
        tiled=True,
    )
    scaled = (gate_weights[0][:, None] * out_share).astype(jnp.bfloat16)
    returned = jnp.dot(
        place_table,
        lax.all_gather(scaled, "dp", axis=0, tiled=True),
        preferred_element_type=jnp.float32,
    )
    sent_back = returned.astype(jnp.bfloat16).reshape(expert_count, MOST, width)
    results = lax.all_to_all(sent_back, EXPERT, split_axis=0, concat_axis=0, tiled=True)
    flat_results = results.reshape(expert_count * MOST, width)
    combined = lax.dot_general(
        pack_table, flat_results, (((0,), (0,)), ((), ())), preferred_element_type=jnp.float32
    )
    return combined.astype(jnp.bfloat16)


def solution(mesh):
    split = Mesh(
        mesh.devices.reshape(mesh.shape["dp"], 4, 4, 2), ("dp", "expert_0", "expert_1", "expert_2")
    )
    placed = (
        P(DP_EXPERT, None),
        P(None, DP_EXPERT),
        P(),
        P(EXPERT, None, "dp"),
        P(EXPERT, "dp", None),
        P(EXPERT, "dp"),
    )
    return jax.shard_map(
        on_device, mesh=split, in_specs=placed, out_specs=P(DP_EXPERT, None), check_vma=False
    )
```

profile of v0, /device:TPU:1, one launch (start us, length us, event | category | flops | bytes accessed | tf_op | source)
XLA Modules:
  0.0 387.2 jit_solution(9165938855514273906)
XLA Ops:
  6.5 0.1 iota.40
  6.6 1.0 convert_reduce_fusion
  7.7 0.6 reduce-window.15
  8.3 0.2 slice_reduce_fusion
  8.6 1.5 fusion.5
  10.0 8.6 %all-to-all-start = ((bf16[32,8,2048]{2,1,0:T(8,128)(2,1)}), bf16[32,8,2048]{2,1,0:T(8,128)(2,1)S(1)}, u32[]{:S(2)}, u32[]{:S(2)}) async-start(bf16[32,8,2048]{2,1,0:T(8,128)(2,1)} %fusion.5), calls=%async_computation | async-start | bytes 2097152 | tf_op jit(solution)/shard_map/all_to_all | solution.py:45
  18.7 0.7 dynamic-slice
  20.1 0.2 dynamic-update-slice
  20.3 15.2 %all-reduce = s32[128]{0:T(128)S(1)} all-reduce(s32[128]{0:T(128)S(1)} %dynamic-update-slice), channel_id=2, replica_groups=mesh['dp'=8,'expert_0'=4,'expert_1'=4,'expert_2'=2] {'expert_0'}, use_global_device_ids=true, to_apply=%add | all-reduce | flops 128 | bytes 1024
  35.5 0.1 reshape.95
  35.6 19.8 %all_gather.16 = s32[32,1,32]{2,1,0:T(1,128)S(1)} all-gather(s32[4,1,32]{2,1,0:T(1,128)S(1)} %bitcast.53), channel_id=1, replica_groups=mesh['dp'=8,'expert_0'=4,'expert_1'=4,'expert_2'=2] {'dp'}, dimensions={0}, use_global_device_ids=true | all-gather | bytes 4608 | tf_op jit(solution)/shard_map/all_gather | solution.py:21
  55.4 9.1 %all_gather.17 = s32[128,1,32]{2,1,0:T(1,128)S(1)} all-gather(s32[32,1,32]{2,1,0:T(1,128)S(1)} %all_gather.16), channel_id=1, replica_groups=mesh['dp'=8,'expert_0'=4,'expert_1'=4,'expert_2'=2] {'expert_1'}, dimensions={0}, use_global_device_ids=true | all-gather | bytes 20480 | tf_op jit(solution)/shard_map/all_gather | solution.py:21
  64.6 12.1 %all_gather.18 = s32[256,1,32]{0,2,1:T(8,128)S(1)} all-gather(s32[128,1,32]{0,2,1:T(8,128)S(1)} %copy.28), channel_id=1, replica_groups=mesh['dp'=8,'expert_0'=4,'expert_1'=4,'expert_2'=2] {'expert_2'}, dimensions={0}, use_global_device_ids=true | all-gather | bytes 49152 | tf_op jit(solution)/shard_map/all_gather | solution.py:21
  76.7 0.1 copy.29
  76.8 1.2 multiply_reduce_fusion
  78.0 0.3 copy.30
  78.3 0.2 reduce_sum.25
  78.5 0.1 reshape.90
  78.6 0.3 reduce-window.19
  79.1 0.1 slice_reduce_fusion.1
  79.4 0.1 add.32
  79.6 0.1 lt.30
  79.7 3.4 convolution_convert_fusion
  83.2 103.9 %all-reduce.3.cloned.1.call-done = bf16[1024,2048]{1,0:T(8,128)(2,1)} async-done(((bf16[1024,2048]{1,0:T(8,128)(2,1)}), bf16[1024,2048]{1,0:T(8,128)(2,1)}) %all-reduce.3.cloned.1.call-update) | async-done | bytes 4194320 | tf_op jit(solution)/shard_map/psum | solution.py:70
  187.1 8.1 %maximum_convert_fusion = bf16[1024,1024]{1,0:T(8,128)(2,1)S(1)} fusion(bf16[1024,2048]{1,0:T(8,128)(2,1)} %all-reduce.3.cloned.1.call-done, bf16[1,2048,1024]{2,1,0:T(8,128)(2,1)} %param.9), kind=kOutput, calls=%fused_computation.4 | convolution fusion | flops 4297064448 | bytes 10485760 | tf_op jit(solution)/shard_map/dot_general | solution.py:72
  195.2 6.7 %fusion = f32[1024,2048]{1,0:T(8,128)} fusion(bf16[1024,1024]{1,0:T(8,128)(2,1)S(1)} %maximum_convert_fusion, bf16[1,1024,2048]{2,1,0:T(8,128)(2,1)S(1)} %copy-done.2), kind=kOutput, calls=%fused_computation | convolution fusion | flops 4294967296 | bytes 14680064 | tf_op jit(solution)/shard_map/dot_general | solution.py:75
  201.9 93.8 %reduce-scatter.2.cloned.1.call-done = f32[128,2048]{1,0:T(8,128)} async-done(((f32[1024,2048]{1,0:T(8,128)}), f32[128,2048]{1,0:T(8,128)}) %reduce-scatter.2.cloned.1.call-update) | async-done | bytes 1048592 | tf_op jit(solution)/shard_map/reduce_scatter | solution.py:74
  295.8 2.1 multiply_convert_fusion
  297.9 53.4 %all-gather.3.cloned.1.call-done = bf16[1024,2048]{1,0:T(8,128)(2,1)} async-done(((bf16[128,2048]{1,0:T(8,128)(2,1)}), bf16[1024,2048]{1,0:T(8,128)(2,1)}) %all-gather.3.cloned.1.call-update) | async-done | bytes 4194320 | tf_op jit(solution)/shard_map/all_gather | solution.py:83
  351.4 3.5 fusion.6
  354.8 24.4 %all_to_all.10 = bf16[32,8,2048]{2,1,0:T(8,128)(2,1)S(1)} all-to-all(bf16[32,8,2048]{2,1,0:T(8,128)(2,1)S(1)} %fusion.6), channel_id=1, replica_groups=mesh['dp'=8,'expert_0'=4,'expert_1'=4,'expert_2'=2] {'expert_0','expert_..., dimensions={0} | all-to-all | bytes 2097152 | tf_op jit(solution)/shard_map/all_to_all | solution.py:87
  379.2 1.5 fusion.4
  (31 shorter events, 0.9 us)
Async XLA Ops:
  6.5 2.0 copy-start
  6.5 12.1 %copy-start.3 = (u32[256]{0:T(256)S(1)}, u32[256]{0:T(256)}, u32[]{:S(2)}) copy-start(u32[256]{0:T(256)} %constant.41) | copy-start | bytes 3076
  10.0 69.7 %all-to-all-start = ((bf16[32,8,2048]{2,1,0:T(8,128)(2,1)}), bf16[32,8,2048]{2,1,0:T(8,128)(2,1)S(1)}, u32[]{:S(2)}, u32[]{:S(2)}) async-start(bf16[32,8,2048]{2,1,0:T(8,128)(2,1)} %fusion.5), calls=%async_computation | async-start | bytes 2097152 | tf_op jit(solution)/shard_map/all_to_all | solution.py:45
  18.6 168.5 %all-reduce.3.cloned.1.call-start = ((), (), s32[]{:S(2)}) async-start(), calls=%async_computation.3 | async-start | bytes 8388608 | tf_op jit(solution)/shard_map/psum | solution.py:70
  83.1 212.6 %reduce-scatter.2.cloned.1.call-start = ((), (), s32[]{:S(2)}) async-start(), calls=%async_computation.4 | async-start | bytes 9437184 | tf_op jit(solution)/shard_map/reduce_scatter | solution.py:74
  187.1 8.1 %copy-start.2 = (bf16[1,1024,2048]{2,1,0:T(8,128)(2,1)S(1)}, bf16[1,1024,2048]{2,1,0:T(8,128)(2,1)}, u32[]{:S(2)}) copy-start(bf16[1,1024,2048]{2,1,0:T(8,128)(2,1)} %param.10) | copy-start | bytes 12582916
  201.8 93.9 %copy-start.1 = (f32[1,128]{1,0:T(1,128)S(1)}, f32[1,128]{1,0:T(1,128)}, u32[]{:S(2)}) copy-start(f32[1,128]{1,0:T(1,128)} %param.11) | copy-start | bytes 1540
  201.9 149.5 %all-gather.3.cloned.1.call-start = ((), (), s32[]{:S(2)}) async-start(), calls=%async_computation.5 | async-start | bytes 4718592 | tf_op jit(solution)/shard_map/all_gather | solution.py:83
Sparse Core Ops, SparseCore 0:
  83.2 103.8 all-reduce.2
  202.0 93.7 reduce-scatter.1
  298.0 53.2 all-gather.2
where the time goes:
time: 388 us; the launch traced here: 387 us
  waiting for transfers between devices  251 us (65%)
  blocking collectives  80.7 us (21%)
  matrix products  24.5 us (6%)
  between operations  14 us (4%)
  starting transfers between devices  8.7 us (2%)
  other arithmetic  5.45 us (1%)
    psum x1, waiting for transfers between devices, on_device(): lax.psum(local_rows, 'dp').astype(jnp.float32).astype(jnp.bfloat16)  104 us
    reduce_scatter x1, waiting for transfers between devices, on_device(): lax.psum_scatter(jnp.dot(hidden, second_weight, preferred_element_type=jn...  93.8 us
    all_gather x1, waiting for transfers between devices, on_device(): lax.all_gather(scaled, 'dp', axis=0, tiled=True)  53.4 us
    all_gather x3, blocking collectives, gather_in_order(): blocks = lax.all_gather(blocks, axes[k], axis=0, tiled=True)  41.1 us
    all_to_all x1, blocking collectives, on_device(): lax.all_to_all(sent_back, EXPERT, split_axis=0, concat_axis=0, tiled=True)  24.4 us
    unnamed x1, blocking collectives  15.2 us
    all_to_all x1, starting transfers between devices, on_device(): lax.all_to_all(packed.reshape(expert_count, MOST, width), EXPERT, split_a...  8.58 us
    dot_general x1, matrix products, on_device(): jnp.dot(slot_rows, first_weight, preferred_element_type=jnp.float32)  8.08 us
  transfers between devices with their start and end apart: 4, of which 3 were waited for; matrix products, arithmetic and copies ran while one was open for 1% of the time, Pallas kernels for 0%

commit v1 on v0

v1 whole, which is shorter than its diff:
```python
import functools
import jax
import jax.numpy as jnp
from jax import lax
from jax.experimental import pallas as pl
from jax.experimental.pallas import tpu as pltpu
from jax.sharding import PartitionSpec as P

MOST = 8
CHUNKS = 4
PLACE_IN_F = {2: 0, 1: 1, 3: 2, 0: 3, 4: 4, 5: 5, 7: 6, 6: 7}
MESH_ID = pl.DeviceIdType.MESH
BF16 = jnp.bfloat16
F32 = jnp.float32


def ring_kernel(
    arrived, row_target, col_target, gate, w_in_hbm, w_out_hbm, out,
    w_in, w_out, own, from_left, from_right, final, hidden, part,
    back_left, back_right, stage_right, stage_left, scaled,
    w_sem, send_sem, recv_sem, back_send_sem, back_recv_sem,
):
    ring = lax.axis_size("dp")
    me = lax.axis_index("dp")
    right = lax.rem(me + 1, ring)
    left = lax.rem(me + ring - 1, ring)
    block = own.shape[2]
    cols = own.shape[3]
    half = CHUNKS // 2
    every = tuple(range(CHUNKS))
    low, high = every[:half], every[half:]
    started = []

    in_copy = pltpu.make_async_copy(w_in_hbm, w_in, w_sem.at[0])
    out_copy = pltpu.make_async_copy(w_out_hbm, w_out, w_sem.at[1])
    in_copy.start()
    out_copy.start()

    barrier = pltpu.get_barrier_semaphore()
    for other in (left, right):
        pl.semaphore_signal(barrier, inc=1, device_id={"dp": other}, device_id_type=MESH_ID)
    pl.semaphore_wait(barrier, 2)

    def copy(src, dst, sends, recvs, way, step, c):
        return pltpu.make_async_remote_copy(
            src_ref=src,
            dst_ref=dst.at[step - 1, c],
            send_sem=sends.at[way, step - 1, c],
            recv_sem=recvs.at[way, step - 1, c],
            device_id={"dp": right if way == 0 else left},
            device_id_type=MESH_ID,
        )

    def send(src, way, step, c):
        sent = copy(src, from_left if way == 0 else from_right, send_sem, recv_sem, way, step, c)
        sent.start()
        started.append(sent)

    def arrive(way, step, c):
        into = from_left if way == 0 else from_right
        copy(into.at[step - 1, c], into, send_sem, recv_sem, way, step, c).wait_recv()
        return into.at[step - 1, c]

    def send_back(src, way, step, c):
        sent = copy(
            src, back_left if way == 0 else back_right, back_send_sem, back_recv_sem, way, step, c
        )
        sent.start()
        started.append(sent)

    def arrive_back(way, step, c):
        into = back_left if way == 0 else back_right
        copy(into.at[step - 1, c], into, back_send_sem, back_recv_sem, way, step, c).wait_recv()

    def at(k, c):
        return pl.ds(PLACE_IN_F[k] * block, block), pl.ds(c * cols, cols)

    def one_hot(k):
        rows = lax.broadcasted_iota(jnp.int32, (block, arrived.shape[0]), 0) + (4 - k) * block
        return (row_target[0:1, :] == rows).astype(F32).astype(BF16)

    def place(k, c, table):
        own[k, c] = jnp.dot(
            table, arrived[:, pl.ds(c * cols, cols)], preferred_element_type=F32
        ).astype(BF16)

    first, last = one_hot(0), one_hot(4)
    for c in every:
        place(0, c, first)
        send(own.at[0, c], 0, 1, c)
        place(4, c, last)
        send(own.at[4, c], 1, 1, c)
    for k in (1, 3, 2):
        table = one_hot(k)
        for c in every:
            place(k, c, table)

    def experts(low_k, count):
        row = PLACE_IN_F[low_k] * block
        rows = count * block
        tile = min(256, w_in.shape[1])

        @pl.loop(0, w_in.shape[1] // tile)
        def _(n):
            at_n = pl.ds(pl.multiple_of(n * tile, tile), tile)
            total = jnp.dot(final[pl.ds(row, rows), :], w_in[:, at_n], preferred_element_type=F32)
            hidden[pl.ds(0, rows), at_n] = jnp.maximum(total, 0.0).astype(BF16)

        @pl.loop(0, w_out.shape[1] // tile)
        def _(n):
            at_n = pl.ds(pl.multiple_of(n * tile, tile), tile)
            part[pl.ds(row, rows), at_n] = jnp.dot(
                hidden[pl.ds(0, rows), :], w_out[:, at_n], preferred_element_type=F32
            )

    for step in range(1, 5):
        for c in every:
            ref = arrive(0, step, c)
            value = ref[...]
            total = value + own[step, c]
            ref[...] = total
            send(ref, 0, step + 1, c)
            if step == 3:
                final[at(3, c)] = value + from_right[0, c]
            if step == 4:
                final[at(4, c)] = total
            ref = arrive(1, step, c)
            value = ref[...]
            total = value + own[4 - step, c]
            ref[...] = total
            send(ref, 1, step + 1, c)
            if step == 2:
                final[at(2, c)] = value + from_left[1, c]
            if step == 3:
                final[at(1, c)] = value + from_left[0, c]
            if step == 4:
                final[at(0, c)] = total
        if step == 3:
            in_copy.wait()
            out_copy.wait()
            experts(2, 3)
        if step == 4:
            experts(0, 2)
    for c in every:
        ref = arrive(0, 5, c)
        if c in low:
            send(ref, 0, 6, c)
        final[at(5, c)] = ref[...]
        ref = arrive(1, 5, c)
        if c in high:
            send(ref, 1, 6, c)
        final[at(7, c)] = ref[...]
    experts(5, 2)
    for c in high:
        stage_right[1, c] = part[at(7, c)].astype(BF16)
        send_back(stage_right.at[1, c], 0, 2, c)
    for c in low:
        stage_left[1, c] = part[at(5, c)].astype(BF16)
        send_back(stage_left.at[1, c], 1, 2, c)
    for c in low:
        final[at(6, c)] = arrive(0, 6, c)[...]
    for c in high:
        final[at(6, c)] = arrive(1, 6, c)[...]
    experts(6, 1)
    for c in low:
        stage_right[0, c] = part[at(6, c)].astype(BF16)
        send_back(stage_right.at[0, c], 0, 1, c)
    for c in high:
        stage_left[0, c] = part[at(6, c)].astype(BF16)
        send_back(stage_left.at[0, c], 1, 1, c)
    for c in low:
        arrive_back(0, 1, c)
        stage_right[1, c] = (part[at(7, c)] + back_left[0, c].astype(F32)).astype(BF16)
        send_back(stage_right.at[1, c], 0, 2, c)
    for c in high:
        arrive_back(1, 1, c)
        stage_left[1, c] = (part[at(5, c)] + back_right[0, c].astype(F32)).astype(BF16)
        send_back(stage_left.at[1, c], 1, 2, c)

    def finish(k, c, total):
        rows = pl.ds((4 - k) * block, block)
        scaled[rows, pl.ds(c * cols, cols)] = (gate[rows, 0:1] * total).astype(BF16)

    for step in range(2, 7):
        for c in every:
            k = step - 2
            arrive_back(0, step, c)
            total = part[at(k, c)] + back_left[step - 1, c].astype(F32)
            if step < 6:
                stage_right[step, c] = total.astype(BF16)
                send_back(stage_right.at[step, c], 0, step + 1, c)
            if step == 5:
                finish(3, c, total + back_right[2, c].astype(F32))
            if step == 6:
                finish(4, c, total + back_right[1, c].astype(F32))
            k = 6 - step
            arrive_back(1, step, c)
            total = part[at(k, c)] + back_right[step - 1, c].astype(F32)
            if step < 6:
                stage_left[step, c] = total.astype(BF16)
                send_back(stage_left.at[step, c], 1, step + 1, c)
            if step == 4:
                finish(2, c, total + back_left[3, c].astype(F32))
            if step == 5:
                finish(1, c, total + back_left[2, c].astype(F32))
            if step == 6:
                finish(0, c, total + back_left[1, c].astype(F32))
    window = 5 * block
    table = (
        col_target[:, 0:1] == lax.broadcasted_iota(jnp.int32, (arrived.shape[0], window), 1)
    ).astype(F32).astype(BF16)
    for c in every:
        at_c = pl.ds(c * cols, cols)
        out[:, at_c] = jnp.dot(table, scaled[:, at_c], preferred_element_type=F32).astype(BF16)
    for sent in started:
        sent.wait_send()


def ring_stage(arrived, row_target, col_target, gate, w_in, w_out):
    rows, width = arrived.shape
    block = rows // 2
    cols = width // CHUNKS
    units = w_in.shape[1]
    slots = (6, CHUNKS, block, cols)
    vmem = pl.BlockSpec(memory_space=pltpu.VMEM)
    anywhere = pl.BlockSpec(memory_space=pl.ANY)
    sems = pltpu.SemaphoreType.DMA((2, 6, CHUNKS))
    return pl.pallas_call(
        ring_kernel,
        out_shape=jax.ShapeDtypeStruct((rows, width), BF16),
        in_specs=[vmem] * 4 + [anywhere] * 2,
        out_specs=vmem,
        scratch_shapes=[
            pltpu.VMEM(w_in.shape, BF16),
            pltpu.VMEM(w_out.shape, BF16),
            pltpu.VMEM((5, CHUNKS, block, cols), BF16),
            pltpu.VMEM(slots, BF16),
            pltpu.VMEM(slots, BF16),
            pltpu.VMEM((8 * block, width), BF16),
            pltpu.VMEM((3 * block, units), BF16),
            pltpu.VMEM((8 * block, width), F32),
            pltpu.VMEM(slots, BF16),
            pltpu.VMEM(slots, BF16),
            pltpu.VMEM(slots, BF16),
            pltpu.VMEM(slots, BF16),
            pltpu.VMEM((5 * block, width), BF16),
            pltpu.SemaphoreType.DMA((2,)),
            sems, sems, sems, sems,
        ],
        compiler_params=pltpu.CompilerParams(
            collective_id=0, has_side_effects=True, vmem_limit_bytes=62 * 1024 * 1024
        ),
        name="ring",
    )(arrived, row_target, col_target, gate, w_in, w_out)


def placement(arrived_counts, plane_counts, me, block):
    planes = plane_counts.shape[0]
    index = lax.broadcasted_iota(jnp.int32, (planes,), 0)
    spare = 2 * block - plane_counts
    left_over = planes * block - jnp.sum(plane_counts)
    padded = plane_counts + jnp.clip(left_over - (jnp.cumsum(spare) - spare), 0, spare)
    drift = jnp.cumsum(padded) - padded - block * index
    mine = index == me
    base = jnp.sum(jnp.where(mine, drift, 0)) - jnp.max(drift) + 4 * block
    first_slot = jnp.sum(jnp.where(index < me, plane_counts, 0))
    starts = jnp.cumsum(arrived_counts) - arrived_counts
    within = lax.broadcasted_iota(jnp.int32, (arrived_counts.shape[0], MOST), 1)
    target = jnp.where(within < arrived_counts[:, None], base + starts[:, None] + within, -1)
    return target.reshape(-1), base, first_slot


def on_device(tokens, expert_ranks, capacity, weight_in, weight_out, gate_weights):
    planes = lax.axis_size("dp")
    expert_count = lax.axis_size("expert")
    me = lax.axis_index("dp")
    token_count, width = tokens.shape
    block = gate_weights.shape[1]
    slots_all = block * planes
    chosen = expert_ranks < capacity[:, None]
    chosen_int = chosen.astype(jnp.int32)
    counts = jnp.sum(chosen_int, axis=1)
    before = jnp.cumsum(chosen_int, axis=1) - chosen_int
    places = lax.broadcasted_iota(jnp.int32, (expert_count, MOST, token_count), 1)
    pack_table = jnp.logical_and(chosen[:, None, :], before[:, None, :] == places)
    pack_table = pack_table.astype(BF16).reshape(expert_count * MOST, token_count)
    packed = jnp.dot(pack_table, tokens, preferred_element_type=F32).astype(BF16)
    arrived_counts = lax.all_to_all(
        counts.reshape(expert_count, 1), "expert", split_axis=0, concat_axis=0, tiled=True
    ).reshape(expert_count)
    plane_counts = lax.all_gather(jnp.sum(arrived_counts), "dp")
    gates = lax.all_gather(gate_weights[0], "dp").reshape(slots_all)
    arrived = lax.all_to_all(
        packed.reshape(expert_count, MOST, width), "expert", split_axis=0, concat_axis=0, tiled=True
    ).reshape(expert_count * MOST, width)
    target, base, first_slot = placement(arrived_counts, plane_counts, me, block)
    slot = first_slot - base + lax.broadcasted_iota(jnp.int32, (5 * block, slots_all), 0)
    slot_ids = lax.broadcasted_iota(jnp.int32, (5 * block, slots_all), 1)
    window_gate = jnp.sum(jnp.where(slot == slot_ids, gates[None, :], 0.0), axis=1)
    returned = ring_stage(
        arrived,
        jnp.broadcast_to(target[None, :], (8, target.shape[0])),
        jnp.broadcast_to(target[:, None], (target.shape[0], 128)),
        jnp.broadcast_to(window_gate[:, None], (5 * block, 128)),
        weight_in[0],
        weight_out[0],
    )
    results = lax.all_to_all(
        returned.reshape(expert_count, MOST, width), "expert", split_axis=0, concat_axis=0, tiled=True
    )
    combined = lax.dot_general(
        pack_table,
        results.reshape(expert_count * MOST, width),
        (((0,), (0,)), ((), ())),
        preferred_element_type=F32,
    )
    return combined.astype(BF16)


def solution(mesh):
    both = ("dp", "expert")
    placed = (
        P(both, None),
        P(None, both),
        P(),
        P("expert", None, "dp"),
        P("expert", "dp", None),
        P("expert", "dp"),
    )
    return jax.shard_map(
        on_device, mesh=mesh, in_specs=placed, out_specs=P(both, None), check_vma=False
    )
```

time: 388 us -> 220 us (0.57)
  waiting for transfers between devices: 251 us -> 0.82 us
  Pallas kernels: 0 us -> 130 us
  blocking collectives: 80.7 us -> 51.3 us
  matrix products: 24.5 us -> 2.91 us
  between operations: 14 us -> 2.56 us
  starting transfers between devices: 8.7 us -> 19.8 us
    pallas_call x0 -> x1, Pallas kernels: none -> 130 us  [ring_stage(): pl.pallas_call(ring_kernel, out_shape=jax.ShapeDtypeStruct((rows, width),...]
    psum x1 -> x0, waiting for transfers between devices: 104 us -> none  [on_device(): lax.psum(local_rows, 'dp').astype(jnp.float32).astype(jnp.bfloat16)]
    reduce_scatter x1 -> x0, waiting for transfers between devices: 93.8 us -> none  [on_device(): lax.psum_scatter(jnp.dot(hidden, second_weight, preferred_element_type=jn...]
    all_gather x1 -> x0, waiting for transfers between devices: 53.4 us -> none  [on_device(): lax.all_gather(scaled, 'dp', axis=0, tiled=True)]
    all_gather x3 -> x1, blocking collectives: 41.1 us -> 15.6 us  [on_device(): gates = lax.all_gather(gate_weights[0], 'dp').reshape(slots_all)]
    dot_general x6 -> x2, matrix products: 24.5 us -> 2.91 us  [the longest x1 1.46 us: on_device(): lax.dot_general(pack_table, results.reshape(expert_count * MOST, width),...]
    all_to_all x1 -> x2, starting transfers between devices: 8.58 us -> 19.8 us  [the longest x1 11.2 us: on_device(): lax.all_to_all(packed.reshape(expert_count, MOST, width), 'expert', split...]
    unnamed x1, blocking collectives: 15.2 us -> 8.38 us
  transfers between devices with their start and end apart: 4 -> 2, of which waited for: 3 -> 1; matrix products, arithmetic and copies ran while one was open for 1% -> 4% of each run, Pallas kernels for 0% -> 0%
where the time goes in v1:
time: 220 us; the launch traced here: 219 us
  Pallas kernels  130 us (59%)
  blocking collectives  51.3 us (23%)
  starting transfers between devices  19.8 us (9%)
  local copies, waits for them, and re-layouts  6.21 us (3%)
  other arithmetic  5.32 us (2%)
  matrix products  2.91 us (1%)
  between operations  2.56 us (1%)
    pallas_call x1, Pallas kernels, ring_stage(): pl.pallas_call(ring_kernel, out_shape=jax.ShapeDtypeStruct((rows, width),...  130 us
    all_to_all x1, blocking collectives, on_device(): lax.all_to_all(returned.reshape(expert_count, MOST, width), 'expert', spl...  27.4 us
    all_gather x1, blocking collectives, on_device(): gates = lax.all_gather(gate_weights[0], 'dp').reshape(slots_all)  15.6 us
    all_to_all x1, starting transfers between devices, on_device(): lax.all_to_all(packed.reshape(expert_count, MOST, width), 'expert', split...  11.2 us
    all_to_all x1, starting transfers between devices, on_device(): lax.all_to_all(counts.reshape(expert_count, 1), 'expert', split_axis=0, c...  8.58 us
    unnamed x1, blocking collectives  8.38 us
  transfers between devices with their start and end apart: 2, of which 1 were waited for; matrix products, arithmetic and copies ran while one was open for 4% of the time, Pallas kernels for 0%

profile of v1, /device:TPU:1, one launch (start us, length us, event | category | flops | bytes accessed | tf_op | source)
XLA Modules:
  0.0 219.2 jit_solution(1907759908578362873)
XLA Ops:
  0.0 1.0 convert_reduce_fusion
  1.0 0.7 copy.25
  1.7 8.6 %all-to-all-start.1 = ((s32[32,1,1]{2,1,0:T(1,128)}), s32[32,1,1]{2,1,0:T(1,128)S(1)}, u32[]{:S(2)}, u32[]{:S(2)}) async-start(s32[32,1,1]{2,1,0:T(1,128)} %copy.25), calls=%async_computation.1 | async-start | bytes 32768 | tf_op jit(solution)/shard_map/all_to_all | solution.py:288
  10.3 0.1 iota.52
  10.4 0.6 reduce-window.36
  11.0 0.2 slice_reduce_fusion
  11.3 0.1 convert_subtract_fusion
  11.3 15.6 %all-gather = f32[8,1,128]{2,1,0:T(1,128)S(1)} all-gather(f32[1,1,128]{2,1,0:T(1,128)} %bitcast.66), channel_id=1, replica_groups=mesh['dp'=8,'expert'=32] {'dp'}, dimensions={0}, use_global_device_ids=true | all-gather | bytes 4608 | tf_op jit(solution)/shard_map/all_gather | solution.py:292
  26.9 1.4 fusion.1
  28.3 1.3 dynamic-slice
  29.7 11.2 %all-to-all-start = ((bf16[32,8,2048]{2,1,0:T(8,128)(2,1)}), bf16[32,8,2048]{2,1,0:T(8,128)(2,1)}, u32[]{:S(2)}, u32[]{:S(2)}) async-start(bf16[32,8,2048]{2,1,0:T(8,128)(2,1)} %fusion.1), calls=%async_computation | async-start | bytes 2097152 | tf_op jit(solution)/shard_map/all_to_all | solution.py:293
  40.9 1.2 fusion.20
  42.1 0.1 lt.35
  42.2 0.1 lt.36
  42.3 0.1 reduce-window.40
  42.3 1.4 dynamic-update-slice
  43.7 0.1 reduce.5
  43.8 8.4 %all-reduce = s32[8]{0:T(128)S(1)} all-reduce(s32[8]{0:T(128)S(1)} %dynamic-update-slice), channel_id=1, replica_groups=mesh['dp'=8,'expert'=32] {'dp'}, use_global_device_ids=true, to_apply=%add | all-reduce | flops 8 | bytes 64
  52.2 0.7 fusion.13
  52.9 0.2 reduce-window.38
  53.6 0.2 reduce-window.39
  53.8 0.7 fusion.19
  55.7 0.1 add.46
  55.8 0.1 add.47
  56.6 0.4 select_reduce_fusion
  57.0 0.8 all-to-all-done
  57.9 0.6 broadcast_in_dim.42.row_target
  58.4 0.8 broadcast_in_dim.43.col_target
  59.2 0.9 broadcast_in_dim.47.gate
  60.1 130.3 %ring.1 = bf16[256,2048]{1,0:T(8,128)(2,1)} custom-call(bf16[256,2048]{1,0:T(8,128)(2,1)} %bitcast.3.arrived, s32[8,256]{1,0:T(8,128)} %broadcast_in_dim.42.row_target, s32[256,128]{1,0:T(8,128)} %broadcast_in_dim.43.col_target, f32[640,128]{1,0:T(8,128)} %broadcast_in_dim.47.gate, bf16[2048,1024]{1,0:T(8,128)(2,1)} %bitcast.60, bf16[1024,2048]{1,0:T(8,128)(2,1)} %bitcast.61), custom_call_target="tpu_custom_call" | custom-call | tf_op jit(solution)/shard_map/ring/pallas_call | solution.py:228
  190.4 27.4 %all_to_all.19 = bf16[32,8,2048]{2,1,0:T(8,128)(2,1)S(1)} all-to-all(bf16[32,8,2048]{2,1,0:T(8,128)(2,1)} %bitcast.59), channel_id=1, replica_groups=mesh['dp'=8,'expert'=32] {'expert'}, dimensions={0} | all-to-all | bytes 2097152 | tf_op jit(solution)/shard_map/all_to_all | solution.py:308
  217.8 1.5 fusion
  (12 shorter events, 0.1 us)
Async XLA Ops:
  0.0 26.9 %copy-start = (bf16[256,2048]{1,0:T(8,128)(2,1)S(1)}, bf16[256,2048]{1,0:T(8,128)(2,1)}, u32[]{:S(2)}) copy-start(bf16[256,2048]{1,0:T(8,128)(2,1)} %param.6) | copy-start | bytes 3145732
  1.7 28.0 %all-to-all-start.1 = ((s32[32,1,1]{2,1,0:T(1,128)}), s32[32,1,1]{2,1,0:T(1,128)S(1)}, u32[]{:S(2)}, u32[]{:S(2)}) async-start(s32[32,1,1]{2,1,0:T(1,128)} %copy.25), calls=%async_computation.1 | async-start | bytes 32768 | tf_op jit(solution)/shard_map/all_to_all | solution.py:288
  29.7 28.2 %all-to-all-start = ((bf16[32,8,2048]{2,1,0:T(8,128)(2,1)}), bf16[32,8,2048]{2,1,0:T(8,128)(2,1)}, u32[]{:S(2)}, u32[]{:S(2)}) async-start(bf16[32,8,2048]{2,1,0:T(8,128)(2,1)} %fusion.1), calls=%async_computation | async-start | bytes 2097152 | tf_op jit(solution)/shard_map/all_to_all | solution.py:293

commit v2 on v1

v2 whole, which is shorter than its diff:
```python
import jax
import jax.numpy as jnp
from jax import lax
from jax.experimental import pallas as pl
from jax.experimental.pallas import tpu as pltpu
from jax.sharding import PartitionSpec as P

MOST = 8
CHUNKS = 4
LANES = 128
PLACE_IN_F = {2: 0, 1: 1, 3: 2, 0: 3, 4: 4, 5: 5, 7: 6, 6: 7}
MESH_ID = pl.DeviceIdType.MESH
BF16 = jnp.bfloat16
F32 = jnp.float32


def iota(shape, dim):
    return lax.broadcasted_iota(jnp.int32, shape, dim)


def dot(a, b):
    return jnp.dot(a, b, preferred_element_type=F32)


def table_of(mask):
    return jnp.where(mask, 1.0, 0.0).astype(BF16)


def layer_kernel(
    capacity, tokens, ranks, gate_in, w_in_hbm, w_out_hbm, out,
    w_in, w_out, own, from_left, from_right, final, hidden, part,
    back_left, back_right, stage_right, stage_left, scaled,
    packed, arrived, returned, results, counts_out, counts_in, totals_out, totals_in,
    gates_out, gates_in, window_gate, place_table, target_column, take_table,
    w_sem, send_sem, recv_sem, back_send_sem, back_recv_sem,
    rows_send, rows_recv, out_send, out_recv, small_send, small_recv,
):
    planes = lax.axis_size("dp")
    experts_all = lax.axis_size("expert")
    me = lax.axis_index("dp")
    my_expert = lax.axis_index("expert")
    right = lax.rem(me + 1, planes)
    left = lax.rem(me + planes - 1, planes)
    block = own.shape[2]
    cols = own.shape[3]
    rows_all = experts_all * MOST
    window = 5 * block
    half = CHUNKS // 2
    every = tuple(range(CHUNKS))
    low, high = every[:half], every[half:]
    started = []

    barrier = pltpu.get_barrier_semaphore()

    @pl.loop(1, experts_all)
    def _(i):
        peer = lax.rem(my_expert + i, experts_all)
        pl.semaphore_signal(barrier, inc=1, device_id={"expert": peer}, device_id_type=MESH_ID)

    @pl.loop(1, planes)
    def _(i):
        peer = lax.rem(me + i, planes)
        pl.semaphore_signal(barrier, inc=1, device_id={"dp": peer}, device_id_type=MESH_ID)

    in_copy = pltpu.make_async_copy(w_in_hbm, w_in, w_sem.at[0])
    out_copy = pltpu.make_async_copy(w_out_hbm, w_out, w_sem.at[1])
    in_copy.start()
    out_copy.start()

    def columns(c):
        return pl.ds(c * cols, cols)

    def grouped(value):
        return value.reshape(experts_all, MOST, value.shape[-1])

    def flat(value):
        return value.astype(F32).reshape(rows_all, value.shape[-1])

    def to_all_experts(src_of, dst, sends, recvs):
        @pl.loop(1, experts_all)
        def _(i):
            peer = lax.rem(my_expert + i, experts_all)
            pltpu.make_async_remote_copy(
                src_ref=src_of(peer),
                dst_ref=dst.at[my_expert],
                send_sem=sends,
                recv_sem=recvs,
                device_id={"expert": peer},
                device_id_type=MESH_ID,
            ).start()

    def to_all_planes(src, dst, sends, recvs):
        @pl.loop(1, planes)
        def _(i):
            peer = lax.rem(me + i, planes)
            pltpu.make_async_remote_copy(
                src_ref=src,
                dst_ref=dst.at[me],
                send_sem=sends,
                recv_sem=recvs,
                device_id={"dp": peer},
                device_id_type=MESH_ID,
            ).start()

    def wait_all(ref, count, sem):
        several = ref.at[pl.ds(0, count)]
        pltpu.make_async_copy(several, several, sem).wait()

    limits = jnp.zeros((experts_all, LANES), jnp.int32)
    for e in range(experts_all):
        limits = jnp.where(iota((experts_all, LANES), 0) == e, capacity[e], limits)
    token_count = tokens.shape[0]
    chosen = ranks[...] < limits[:, 0:1]
    chosen_table = table_of(chosen)
    earlier = table_of(iota((token_count, token_count), 0) < iota((token_count, token_count), 1))
    code = jnp.where(chosen, dot(chosen_table, earlier), -1.0).astype(BF16)
    expand = table_of(
        iota((rows_all, experts_all), 0) // MOST == iota((rows_all, experts_all), 1)
    )
    row_counts = dot(
        expand, dot(chosen_table, jnp.ones((token_count, LANES), BF16)).astype(BF16)
    )
    counts_out[...] = grouped(row_counts)
    gates_out[...] = jnp.broadcast_to(gate_in[...], gates_out.shape)
    within = (iota((rows_all, token_count), 0) % MOST).astype(F32)
    pack = jnp.where(dot(expand, code) == within, 1.0, 0.0)
    pack_table = pack.astype(BF16)
    for c in every:
        packed[c] = grouped(dot(pack_table, tokens[:, columns(c)])).astype(BF16)
        arrived[c, my_expert] = packed[c, my_expert]
    counts_in[my_expert] = counts_out[my_expert]
    gates_in[me] = gates_out[...]

    pl.semaphore_wait(barrier, experts_all + planes - 2)
    to_all_experts(lambda peer: counts_out.at[peer], counts_in, small_send.at[0], small_recv.at[0])
    to_all_experts(lambda peer: packed.at[0, peer], arrived.at[0], rows_send.at[0], rows_recv.at[0])

    wait_all(counts_in, experts_all - 1, small_recv.at[0])
    counts = counts_in[...].reshape(rows_all, LANES)
    counts_table = counts.astype(BF16)
    lead = iota((MOST, rows_all), 1) % MOST == 0
    totals_out[...] = dot(table_of(lead), counts_table)
    totals_in[me] = totals_out[...]
    to_all_planes(totals_out, totals_in, small_send.at[1], small_recv.at[1])
    to_all_planes(gates_out, gates_in, small_send.at[2], small_recv.at[2])
    for c in every[1:]:
        to_all_experts(
            lambda peer: packed.at[c, peer], arrived.at[c], rows_send.at[c], rows_recv.at[c]
        )
    row_ids = iota((rows_all, rows_all), 0)
    lane_ids = iota((rows_all, rows_all), 1)
    ahead = jnp.logical_and(lane_ids % MOST == 0, lane_ids // MOST < row_ids // MOST)
    starts = dot(table_of(ahead), counts_table)
    place_in = (iota((rows_all, LANES), 0) % MOST).astype(F32)
    take_table[...] = pack.T.astype(BF16)
    wait_all(totals_in, planes - 1, small_recv.at[1])
    plane_counts = [totals_in[z] for z in range(planes)]
    left_over = jnp.full((MOST, LANES), float(planes * block), F32)
    for z in range(planes):
        left_over = left_over - plane_counts[z]
    padded_start = jnp.zeros((MOST, LANES), F32)
    first_slot = padded_start
    drift_mine = padded_start
    drift_most = padded_start
    for z in range(planes):
        drift = padded_start - float(z * block)
        drift_most = jnp.maximum(drift_most, drift)
        drift_mine = jnp.where(me == z, drift, drift_mine)
        first_slot = first_slot + jnp.where(me > z, plane_counts[z], 0.0)
        extra = jnp.minimum(2.0 * block - plane_counts[z], left_over)
        left_over = left_over - extra
        padded_start = padded_start + plane_counts[z] + extra
    base = drift_mine - drift_most + 4.0 * block
    target = jnp.where(place_in < counts, base[0:1, :] + starts + place_in, -1.0)
    target_column[...] = target
    target_row = target.T[0:1, :]
    place_table[...] = table_of(target_row == iota((window, rows_all), 0).astype(F32))

    def copy(src, dst, sends, recvs, way, step, c):
        return pltpu.make_async_remote_copy(
            src_ref=src,
            dst_ref=dst.at[step - 1, c],
            send_sem=sends.at[way, step - 1, c],
            recv_sem=recvs.at[way, step - 1, c],
            device_id={"dp": right if way == 0 else left},
            device_id_type=MESH_ID,
        )

    def send(src, way, step, c):
        sent = copy(src, from_left if way == 0 else from_right, send_sem, recv_sem, way, step, c)
        sent.start()
        started.append(sent)

    def arrive(way, step, c):
        into = from_left if way == 0 else from_right
        copy(into.at[step - 1, c], into, send_sem, recv_sem, way, step, c).wait_recv()
        return into.at[step - 1, c]

    def send_back(src, way, step, c):
        sent = copy(
            src, back_left if way == 0 else back_right, back_send_sem, back_recv_sem, way, step, c
        )
        sent.start()
        started.append(sent)

    def arrive_back(way, step, c):
        into = back_left if way == 0 else back_right
        copy(into.at[step - 1, c], into, back_send_sem, back_recv_sem, way, step, c).wait_recv()

    def at(k, c):
        return pl.ds(PLACE_IN_F[k] * block, block), columns(c)

    def place(k, c, rows):
        own[k, c] = dot(place_table[pl.ds((4 - k) * block, block), :], rows).astype(BF16)

    def arrived_rows(c):
        return flat(arrived[c]).astype(BF16)

    for c in every:
        wait_all(arrived.at[c], experts_all - 1, rows_recv.at[c])
        rows = arrived_rows(c)
        place(0, c, rows)
        send(own.at[0, c], 0, 1, c)
        place(4, c, rows)
        send(own.at[4, c], 1, 1, c)
        for k in (1, 3, 2):
            place(k, c, rows)

    def experts(low_k, count):
        row = PLACE_IN_F[low_k] * block
        rows = count * block
        tile = min(256, w_in.shape[1])

        @pl.loop(0, w_in.shape[1] // tile)
        def _(n):
            at_n = pl.ds(pl.multiple_of(n * tile, tile), tile)
            total = dot(final[pl.ds(row, rows), :], w_in[:, at_n])
            hidden[pl.ds(0, rows), at_n] = jnp.maximum(total, 0.0).astype(BF16)

        @pl.loop(0, w_out.shape[1] // tile)
        def _(n):
            at_n = pl.ds(pl.multiple_of(n * tile, tile), tile)
            part[pl.ds(row, rows), at_n] = dot(hidden[pl.ds(0, rows), :], w_out[:, at_n])

    for step in range(1, 5):
        for c in every:
            ref = arrive(0, step, c)
            value = ref[...]
            total = value + own[step, c]
            ref[...] = total
            send(ref, 0, step + 1, c)
            if step == 3:
                final[at(3, c)] = value + from_right[0, c]
            if step == 4:
                final[at(4, c)] = total
            ref = arrive(1, step, c)
            value = ref[...]
            total = value + own[4 - step, c]
            ref[...] = total
            send(ref, 1, step + 1, c)
            if step == 2:
                final[at(2, c)] = value + from_left[1, c]
            if step == 3:
                final[at(1, c)] = value + from_left[0, c]
            if step == 4:
                final[at(0, c)] = total
        if step == 1:
            wait_all(gates_in, planes - 1, small_recv.at[2])
            shift = (first_slot - base)[0:1, 0:1]
            gap = (iota((window, block), 1) - iota((window, block), 0)).astype(F32)
            total = jnp.zeros((window, block), F32)
            for z in range(planes):
                total = total + jnp.where(gap + float(z * block) == shift, gates_in[z][0:1, :], 0.0)
            window_gate[...] = jnp.broadcast_to(
                jnp.sum(total, axis=1, keepdims=True), window_gate.shape
            )
        if step == 3:
            in_copy.wait()
            out_copy.wait()
            experts(2, 3)
        if step == 4:
            experts(0, 2)
    for c in every:
        ref = arrive(0, 5, c)
        if c in low:
            send(ref, 0, 6, c)
        final[at(5, c)] = ref[...]
        ref = arrive(1, 5, c)
        if c in high:
            send(ref, 1, 6, c)
        final[at(7, c)] = ref[...]
    experts(5, 2)
    for c in high:
        stage_right[1, c] = part[at(7, c)].astype(BF16)
        send_back(stage_right.at[1, c], 0, 2, c)
    for c in low:
        stage_left[1, c] = part[at(5, c)].astype(BF16)
        send_back(stage_left.at[1, c], 1, 2, c)
    for c in low:
        final[at(6, c)] = arrive(0, 6, c)[...]
    for c in high:
        final[at(6, c)] = arrive(1, 6, c)[...]
    experts(6, 1)
    for c in low:
        stage_right[0, c] = part[at(6, c)].astype(BF16)
        send_back(stage_right.at[0, c], 0, 1, c)
    for c in high:
        stage_left[0, c] = part[at(6, c)].astype(BF16)
        send_back(stage_left.at[0, c], 1, 1, c)
    for c in low:
        arrive_back(0, 1, c)
        stage_right[1, c] = (part[at(7, c)] + back_left[0, c].astype(F32)).astype(BF16)
        send_back(stage_right.at[1, c], 0, 2, c)
    for c in high:
        arrive_back(1, 1, c)
        stage_left[1, c] = (part[at(5, c)] + back_right[0, c].astype(F32)).astype(BF16)
        send_back(stage_left.at[1, c], 1, 2, c)

    def finish(k, c, total):
        rows = pl.ds((4 - k) * block, block)
        scaled[rows, columns(c)] = (window_gate[rows, 0:1] * total).astype(BF16)

    pick_table = table_of(
        target_column[:, 0:1] == iota((rows_all, window), 1).astype(F32)
    )
    for step in range(2, 7):
        for c in every:
            k = step - 2
            arrive_back(0, step, c)
            total = part[at(k, c)] + back_left[step - 1, c].astype(F32)
            if step < 6:
                stage_right[step, c] = total.astype(BF16)
                send_back(stage_right.at[step, c], 0, step + 1, c)
            if step == 5:
                finish(3, c, total + back_right[2, c].astype(F32))
            if step == 6:
                finish(4, c, total + back_right[1, c].astype(F32))
            k = 6 - step
            arrive_back(1, step, c)
            total = part[at(k, c)] + back_right[step - 1, c].astype(F32)
            if step < 6:
                stage_left[step, c] = total.astype(BF16)
                send_back(stage_left.at[step, c], 1, step + 1, c)
            if step == 4:
                finish(2, c, total + back_left[3, c].astype(F32))
            if step == 5:
                finish(1, c, total + back_left[2, c].astype(F32))
            if step == 6:
                finish(0, c, total + back_left[1, c].astype(F32))
                returned[c] = grouped(dot(pick_table, scaled[:, columns(c)])).astype(BF16)
                to_all_experts(
                    lambda peer: returned.at[c, peer], results.at[c], out_send.at[c], out_recv.at[c]
                )
                results[c, my_expert] = returned[c, my_expert]
    for c in every:
        wait_all(results.at[c], experts_all - 1, out_recv.at[c])
        out[:, columns(c)] = dot(take_table[...], flat(results[c]).astype(BF16)).astype(BF16)

    for sent in started:
        sent.wait_send()
    wait_all(counts_out, experts_all - 1, small_send.at[0])
    wait_all(totals_in, planes - 1, small_send.at[1])
    wait_all(gates_in, planes - 1, small_send.at[2])
    for c in every:
        wait_all(packed.at[c], experts_all - 1, rows_send.at[c])
        wait_all(returned.at[c], experts_all - 1, out_send.at[c])


def on_device(tokens, expert_ranks, capacity, weight_in, weight_out, gate_weights):
    planes = lax.axis_size("dp")
    experts_all = lax.axis_size("expert")
    token_count, width = tokens.shape
    block = gate_weights.shape[1]
    units = weight_in.shape[2]
    cols = width // CHUNKS
    rows_all = experts_all * MOST
    vmem = pl.BlockSpec(memory_space=pltpu.VMEM)
    anywhere = pl.BlockSpec(memory_space=pl.ANY)
    slots = pltpu.VMEM((6, CHUNKS, block, cols), BF16)
    exchange = pltpu.VMEM((CHUNKS, experts_all, MOST, cols), BF16)
    ring_sems = pltpu.SemaphoreType.DMA((2, 6, CHUNKS))
    chunk_sems = pltpu.SemaphoreType.DMA((CHUNKS,))
    return pl.pallas_call(
        layer_kernel,
        out_shape=jax.ShapeDtypeStruct((token_count, width), BF16),
        in_specs=[pl.BlockSpec(memory_space=pltpu.SMEM)] + [vmem] * 3 + [anywhere] * 2,
        out_specs=vmem,
        scratch_shapes=[
            pltpu.VMEM(weight_in.shape[1:], BF16),
            pltpu.VMEM(weight_out.shape[1:], BF16),
            pltpu.VMEM((5, CHUNKS, block, cols), BF16),
            slots, slots,
            pltpu.VMEM((8 * block, width), BF16),
            pltpu.VMEM((3 * block, units), BF16),
            pltpu.VMEM((8 * block, width), F32),
            slots, slots, slots, slots,
            pltpu.VMEM((5 * block, width), BF16),
            exchange, exchange, exchange, exchange,
            pltpu.VMEM((experts_all, MOST, LANES), F32),
            pltpu.VMEM((experts_all, MOST, LANES), F32),
            pltpu.VMEM((MOST, LANES), F32),
            pltpu.VMEM((planes, MOST, LANES), F32),
            pltpu.VMEM((MOST, block), F32),
            pltpu.VMEM((planes, MOST, block), F32),
            pltpu.VMEM((5 * block, LANES), F32),
            pltpu.VMEM((5 * block, rows_all), BF16),
            pltpu.VMEM((rows_all, LANES), F32),
            pltpu.VMEM((token_count, rows_all), BF16),
            pltpu.SemaphoreType.DMA((2,)),
            ring_sems, ring_sems, ring_sems, ring_sems,
            chunk_sems, chunk_sems, chunk_sems, chunk_sems,
            pltpu.SemaphoreType.DMA((3,)),
            pltpu.SemaphoreType.DMA((3,)),
        ],
        compiler_params=pltpu.CompilerParams(
            collective_id=0, has_side_effects=True, vmem_limit_bytes=63 * 1024 * 1024
        ),
        name="layer",
    )(capacity, tokens, expert_ranks, gate_weights, weight_in[0], weight_out[0])


def solution(mesh):
    both = ("dp", "expert")
    placed = (
        P(both, None),
        P(None, both),
        P(),
        P("expert", None, "dp"),
        P("expert", "dp", None),
        P("expert", "dp"),
    )
    return jax.shard_map(
        on_device, mesh=mesh, in_specs=placed, out_specs=P(both, None), check_vma=False
    )
```

time: 220 us -> 164 us (0.75)
  blocking collectives: 51.3 us -> 0 us
  Pallas kernels: 130 us -> 162 us
  starting transfers between devices: 19.8 us -> 0 us
  other arithmetic: 5.32 us -> 0 us
  local copies, waits for them, and re-layouts: 6.21 us -> 2.3 us
  matrix products: 2.91 us -> 0 us
  between operations: 2.56 us -> 0.01 us
    pallas_call x1, Pallas kernels: 130 us -> 162 us  [on_device(): pl.pallas_call(layer_kernel, out_shape=jax.ShapeDtypeStruct((token_count,...]
    all_to_all x1 -> x0, blocking collectives: 27.4 us -> none  [on_device(): lax.all_to_all(returned.reshape(expert_count, MOST, width), 'expert', spl...]
    all_to_all x2 -> x0, starting transfers between devices: 19.8 us -> none  [the longest x1 11.2 us: on_device(): lax.all_to_all(packed.reshape(expert_count, MOST, width), 'expert', split...]
    all_gather x1 -> x0, blocking collectives: 15.6 us -> none  [on_device(): gates = lax.all_gather(gate_weights[0], 'dp').reshape(slots_all)]
    unnamed x1 -> x0, blocking collectives: 8.38 us -> none
    reduce_sum x4 -> x0, other arithmetic: 3.38 us -> none  [the longest x1 1.2 us: on_device(): plane_counts = lax.all_gather(jnp.sum(arrived_counts), 'dp')]
    dot_general x2 -> x0, matrix products: 2.91 us -> none  [the longest x1 1.46 us: on_device(): lax.dot_general(pack_table, results.reshape(expert_count * MOST, width),...]
    broadcast_in_dim x3 -> x0, local copies, waits for them, and re-layouts: 2.22 us -> none  [the longest x1 0.87 us: on_device(): jnp.broadcast_to(window_gate[:, None], (5 * block, 128))]
  transfers between devices with their start and end apart: 2 -> 0, of which waited for: 1 -> 0; matrix products, arithmetic and copies ran while one was open for 4% -> 0% of each run, Pallas kernels for 0% -> 0%
where the time goes in v2:
time: 164 us
  Pallas kernels  162 us (99%)
  local copies, waits for them, and re-layouts  2.3 us (1%)
    pallas_call x1, Pallas kernels, on_device(): pl.pallas_call(layer_kernel, out_shape=jax.ShapeDtypeStruct((token_count,...  162 us

profile of v2, /device:TPU:1, one launch (start us, length us, event | category | flops | bytes accessed | tf_op | source)
XLA Modules:
  0.0 163.9 jit_solution(6601913569830445602)
XLA Ops:
  0.0 161.5 %layer.1 = bf16[256,2048]{1,0:T(8,128)(2,1)} custom-call(s32[32]{0:T(128)} %capacity.1, bf16[256,2048]{1,0:T(8,128)(2,1)} %tokens.1, s32[32,256]{1,0:T(8,128)} %ranks.1, f32[1,128]{1,0:T(1,128)} %gate_in.1, bf16[2048,1024]{1,0:T(8,128)(2,1)} %bitcast.2, bf16[1024,2048]{1,0:T(8,128)(2,1)} %bitcast.3), custom_call_target="tpu_custom_call" | custom-call | tf_op jit(solution)/shard_map/layer/pallas_call | solution.py:383
  161.5 2.3 %copy.8 = bf16[256,2048]{1,0:T(8,128)(2,1)} copy(bf16[256,2048]{1,0:T(8,128)(2,1)} %layer.1) | data formatting | bytes 2097152

commit v3 on v2

v3 whole, which is shorter than its diff:
```python
import jax
import jax.numpy as jnp
from jax import lax
from jax.experimental import pallas as pl
from jax.experimental.pallas import tpu as pltpu
from jax.sharding import PartitionSpec as P

MOST = 8
SIXTEENTHS = (4, 4, 4, 2, 2)
FIRST_HALF = 2
LANES = 128
PLACE_IN_F = {2: 0, 1: 1, 3: 2, 0: 3, 4: 4, 5: 5, 7: 6, 6: 7}
MESH_ID = pl.DeviceIdType.MESH
BF16 = jnp.bfloat16
F32 = jnp.float32


def iota(shape, dim):
    return lax.broadcasted_iota(jnp.int32, shape, dim)


def dot(a, b):
    return jnp.dot(a, b, preferred_element_type=F32)


def table_of(mask):
    return jnp.where(mask, 1.0, 0.0).astype(BF16)


def layer_kernel(
    capacity, tokens_hbm, ranks_hbm, gate_hbm, w_in_hbm, w_out_hbm, out,
    tokens, ranks, gate_in, w_in, w_out, own, from_left, from_right, final, hidden, part,
    back_left, back_right, stage_right, stage_left, scaled,
    packed, arrived, returned, results, counts_out, counts_in, counts_flat, totals_out, totals_in,
    gates_out, gates_in, window_gate, place_table, target_column, take_table,
    in_sem, send_sem, recv_sem, back_send_sem, back_recv_sem,
    rows_send, rows_recv, out_send, out_recv, small_send, small_recv,
):
    planes = lax.axis_size("dp")
    experts_all = lax.axis_size("expert")
    me = lax.axis_index("dp")
    my_expert = lax.axis_index("expert")
    right = lax.rem(me + 1, planes)
    left = lax.rem(me + planes - 1, planes)
    block = own.shape[1]
    width = own.shape[2]
    widths = [width // 16 * share for share in SIXTEENTHS]
    rows_all = experts_all * MOST
    window = 5 * block
    every = tuple(range(len(widths)))
    half = FIRST_HALF
    low, high = every[:half], every[half:]
    started = []

    loads = [
        pltpu.make_async_copy(src, dst, in_sem.at[n])
        for n, (src, dst) in enumerate(
            (
                (ranks_hbm, ranks),
                (gate_hbm, gate_in),
                (tokens_hbm, tokens),
                (w_in_hbm, w_in),
                (w_out_hbm, w_out),
            )
        )
    ]
    for load in loads[:3]:
        load.start()

    def partner(i):
        return lax.rem(my_expert + i + 1, experts_all)

    barrier = pltpu.get_barrier_semaphore()

    @pl.loop(0, experts_all - 1)
    def _(i):
        peer = partner(i)
        pl.semaphore_signal(barrier, inc=1, device_id={"expert": peer}, device_id_type=MESH_ID)

    @pl.loop(1, planes)
    def _(i):
        peer = lax.rem(me + i, planes)
        pl.semaphore_signal(barrier, inc=1, device_id={"dp": peer}, device_id_type=MESH_ID)

    def columns(c):
        return pl.ds(sum(widths[:c]), widths[c])

    def grouped(value):
        return value.reshape(experts_all, MOST, value.shape[-1])

    def flat(value):
        return value.astype(F32).reshape(rows_all, value.shape[-1])

    def to_all_experts(src_of, dst, sends, recvs):
        @pl.loop(0, experts_all - 1, unroll=True)
        def _(i):
            peer = partner(i)
            pltpu.make_async_remote_copy(
                src_ref=src_of(peer),
                dst_ref=dst.at[my_expert],
                send_sem=sends,
                recv_sem=recvs,
                device_id={"expert": peer},
                device_id_type=MESH_ID,
            ).start()

    def to_all_planes(src, dst, sends, recvs):
        @pl.loop(1, planes)
        def _(i):
            peer = lax.rem(me + i, planes)
            pltpu.make_async_remote_copy(
                src_ref=src,
                dst_ref=dst.at[me],
                send_sem=sends,
                recv_sem=recvs,
                device_id={"dp": peer},
                device_id_type=MESH_ID,
            ).start()

    def wait_all(ref, count, sem):
        several = ref.at[pl.ds(0, count)]
        pltpu.make_async_copy(several, several, sem).wait()

    def rows_of(ref, c):
        return ref.at[:, :, columns(c)]

    limits = jnp.zeros((experts_all, LANES), jnp.int32)
    for e in range(experts_all):
        limits = jnp.where(iota((experts_all, LANES), 0) == e, capacity[e], limits)
    token_count = tokens.shape[0]
    loads[0].wait()
    chosen = ranks[...] < limits[:, 0:1]
    chosen_table = table_of(chosen)
    taken = dot(chosen_table, jnp.ones((token_count, LANES), BF16))
    for e in range(experts_all):
        counts_out[e] = taken[e : e + 1, :]
    counts_in[my_expert] = counts_out[my_expert]
    loads[1].wait()
    gates_out[...] = jnp.broadcast_to(gate_in[...], gates_out.shape)
    gates_in[me] = gates_out[...]

    pl.semaphore_wait(barrier, experts_all + planes - 2)
    to_all_experts(lambda peer: counts_out.at[peer], counts_in, small_send.at[0], small_recv.at[0])
    to_all_planes(gates_out, gates_in, small_send.at[2], small_recv.at[2])

    earlier = table_of(iota((token_count, token_count), 0) < iota((token_count, token_count), 1))
    code = jnp.where(chosen, dot(chosen_table, earlier), -1.0).astype(BF16)
    expand = table_of(
        iota((rows_all, experts_all), 0) // MOST == iota((rows_all, experts_all), 1)
    )
    within = (iota((rows_all, token_count), 0) % MOST).astype(F32)
    pack = jnp.where(dot(expand, code) == within, 1.0, 0.0)
    pack_table = pack.astype(BF16)

    def pack_rows(c):
        packed[:, :, columns(c)] = grouped(dot(pack_table, tokens[:, columns(c)])).astype(BF16)
        to_all_experts(
            lambda peer: rows_of(packed, c).at[peer],
            rows_of(arrived, c),
            rows_send.at[c],
            rows_recv.at[c],
        )
        arrived[my_expert, :, columns(c)] = packed[my_expert, :, columns(c)]

    loads[2].wait()
    for load in loads[3:]:
        load.start()
    pack_rows(0)
    pack_rows(1)

    wait_all(counts_in, experts_all - 1, small_recv.at[0])
    for e in range(experts_all):
        counts_flat[e : e + 1, :] = counts_in[e]
    counts = dot(expand, counts_flat[...].astype(BF16))
    totals_out[...] = jnp.broadcast_to(
        jnp.sum(counts_flat[...], axis=0, keepdims=True), totals_out.shape
    )
    to_all_planes(totals_out, totals_in, small_send.at[1], small_recv.at[1])
    totals_in[me] = totals_out[...]
    for c in every[2:]:
        pack_rows(c)
    counts_table = counts.astype(BF16)
    row_ids = iota((rows_all, rows_all), 0)
    lane_ids = iota((rows_all, rows_all), 1)
    ahead = jnp.logical_and(lane_ids % MOST == 0, lane_ids // MOST < row_ids // MOST)
    starts = dot(table_of(ahead), counts_table)
    place_in = (iota((rows_all, LANES), 0) % MOST).astype(F32)
    take_table[...] = pack.T.astype(BF16)
    wait_all(totals_in, planes - 1, small_recv.at[1])
    plane_counts = [totals_in[z] for z in range(planes)]
    left_over = jnp.full((MOST, LANES), float(planes * block), F32)
    for z in range(planes):
        left_over = left_over - plane_counts[z]
    padded_start = jnp.zeros((MOST, LANES), F32)
    first_slot = padded_start
    drift_mine = padded_start
    drift_most = padded_start
    for z in range(planes):
        drift = padded_start - float(z * block)
        drift_most = jnp.maximum(drift_most, drift)
        drift_mine = jnp.where(me == z, drift, drift_mine)
        first_slot = first_slot + jnp.where(me > z, plane_counts[z], 0.0)
        extra = jnp.minimum(2.0 * block - plane_counts[z], left_over)
        left_over = left_over - extra
        padded_start = padded_start + plane_counts[z] + extra
    base = drift_mine - drift_most + 4.0 * block
    target = jnp.where(place_in < counts, base[0:1, :] + starts + place_in, -1.0)
    target_column[...] = target
    target_row = target.T[0:1, :]
    place_table[...] = table_of(target_row == iota((window, rows_all), 0).astype(F32))

    def copy(src, dst, sends, recvs, way, step, c):
        return pltpu.make_async_remote_copy(
            src_ref=src,
            dst_ref=dst.at[step - 1, :, columns(c)],
            send_sem=sends.at[way, step - 1, c],
            recv_sem=recvs.at[way, step - 1, c],
            device_id={"dp": right if way == 0 else left},
            device_id_type=MESH_ID,
        )

    def send(src, way, step, c):
        sent = copy(src, from_left if way == 0 else from_right, send_sem, recv_sem, way, step, c)
        sent.start()
        started.append(sent)

    def arrive(way, step, c):
        into = from_left if way == 0 else from_right
        ref = into.at[step - 1, :, columns(c)]
        copy(ref, into, send_sem, recv_sem, way, step, c).wait_recv()
        return ref

    def send_back(src, way, step, c):
        sent = copy(
            src, back_left if way == 0 else back_right, back_send_sem, back_recv_sem, way, step, c
        )
        sent.start()
        started.append(sent)

    def arrive_back(way, step, c):
        into = back_left if way == 0 else back_right
        ref = into.at[step - 1, :, columns(c)]
        copy(ref, into, back_send_sem, back_recv_sem, way, step, c).wait_recv()

    def at(k, c):
        return pl.ds(PLACE_IN_F[k] * block, block), columns(c)

    def place(k, c, rows):
        own[k, :, columns(c)] = dot(place_table[pl.ds((4 - k) * block, block), :], rows).astype(BF16)

    def arrived_rows(c):
        return flat(arrived[:, :, columns(c)]).astype(BF16)

    for c in every:
        wait_all(rows_of(arrived, c), experts_all - 1, rows_recv.at[c])
        rows = arrived_rows(c)
        place(0, c, rows)
        send(own.at[0, :, columns(c)], 0, 1, c)
        place(4, c, rows)
        send(own.at[4, :, columns(c)], 1, 1, c)
        for k in (1, 3, 2):
            place(k, c, rows)

    def experts(low_k, count):
        row = PLACE_IN_F[low_k] * block
        rows = count * block
        tile = min(256, w_in.shape[1])

        @pl.loop(0, w_in.shape[1] // tile)
        def _(n):
            at_n = pl.ds(pl.multiple_of(n * tile, tile), tile)
            total = dot(final[pl.ds(row, rows), :], w_in[:, at_n])
            hidden[pl.ds(0, rows), at_n] = jnp.maximum(total, 0.0).astype(BF16)

        @pl.loop(0, w_out.shape[1] // tile)
        def _(n):
            at_n = pl.ds(pl.multiple_of(n * tile, tile), tile)
            part[pl.ds(row, rows), at_n] = dot(hidden[pl.ds(0, rows), :], w_out[:, at_n])

    for step in range(1, 5):
        for c in every:
            ref = arrive(0, step, c)
            value = ref[...]
            total = value + own[step, :, columns(c)]
            ref[...] = total
            send(ref, 0, step + 1, c)
            if step == 3:
                final[at(3, c)] = value + from_right[0, :, columns(c)]
            if step == 4:
                final[at(4, c)] = total
            ref = arrive(1, step, c)
            value = ref[...]
            total = value + own[4 - step, :, columns(c)]
            ref[...] = total
            send(ref, 1, step + 1, c)
            if step == 2:
                final[at(2, c)] = value + from_left[1, :, columns(c)]
            if step == 3:
                final[at(1, c)] = value + from_left[0, :, columns(c)]
            if step == 4:
                final[at(0, c)] = total
        if step == 1:
            wait_all(gates_in, planes - 1, small_recv.at[2])
            shift = (first_slot - base)[0:1, 0:1]
            gap = (iota((window, block), 1) - iota((window, block), 0)).astype(F32)
            total = jnp.zeros((window, block), F32)
            for z in range(planes):
                total = total + jnp.where(gap + float(z * block) == shift, gates_in[z][0:1, :], 0.0)
            window_gate[...] = jnp.broadcast_to(
                jnp.sum(total, axis=1, keepdims=True), window_gate.shape
            )
        if step == 3:
            loads[3].wait()
            loads[4].wait()
            experts(2, 3)
        if step == 4:
            experts(0, 2)
    for c in every:
        ref = arrive(0, 5, c)
        if c in low:
            send(ref, 0, 6, c)
        final[at(5, c)] = ref[...]
        ref = arrive(1, 5, c)
        if c in high:
            send(ref, 1, 6, c)
        final[at(7, c)] = ref[...]
    experts(5, 2)
    for c in high:
        stage_right[1, :, columns(c)] = part[at(7, c)].astype(BF16)
        send_back(stage_right.at[1, :, columns(c)], 0, 2, c)
    for c in low:
        stage_left[1, :, columns(c)] = part[at(5, c)].astype(BF16)
        send_back(stage_left.at[1, :, columns(c)], 1, 2, c)
    for c in low:
        final[at(6, c)] = arrive(0, 6, c)[...]
    for c in high:
        final[at(6, c)] = arrive(1, 6, c)[...]
    experts(6, 1)
    for c in low:
        stage_right[0, :, columns(c)] = part[at(6, c)].astype(BF16)
        send_back(stage_right.at[0, :, columns(c)], 0, 1, c)
    for c in high:
        stage_left[0, :, columns(c)] = part[at(6, c)].astype(BF16)
        send_back(stage_left.at[0, :, columns(c)], 1, 1, c)
    for c in low:
        arrive_back(0, 1, c)
        stage_right[1, :, columns(c)] = (part[at(7, c)] + back_left[0, :, columns(c)].astype(F32)).astype(BF16)
        send_back(stage_right.at[1, :, columns(c)], 0, 2, c)
    for c in high:
        arrive_back(1, 1, c)
        stage_left[1, :, columns(c)] = (part[at(5, c)] + back_right[0, :, columns(c)].astype(F32)).astype(BF16)
        send_back(stage_left.at[1, :, columns(c)], 1, 2, c)

    def finish(k, c, total):
        rows = pl.ds((4 - k) * block, block)
        scaled[rows, columns(c)] = (window_gate[rows, 0:1] * total).astype(BF16)

    pick_table = table_of(
        target_column[:, 0:1] == iota((rows_all, window), 1).astype(F32)
    )
    for step in range(2, 7):
        for c in every:
            k = step - 2
            arrive_back(0, step, c)
            total = part[at(k, c)] + back_left[step - 1, :, columns(c)].astype(F32)
            if step < 6:
                stage_right[step, :, columns(c)] = total.astype(BF16)
                send_back(stage_right.at[step, :, columns(c)], 0, step + 1, c)
            if step == 5:
                finish(3, c, total + back_right[2, :, columns(c)].astype(F32))
            if step == 6:
                finish(4, c, total + back_right[1, :, columns(c)].astype(F32))
            k = 6 - step
            arrive_back(1, step, c)
            total = part[at(k, c)] + back_right[step - 1, :, columns(c)].astype(F32)
            if step < 6:
                stage_left[step, :, columns(c)] = total.astype(BF16)
                send_back(stage_left.at[step, :, columns(c)], 1, step + 1, c)
            if step == 4:
                finish(2, c, total + back_left[3, :, columns(c)].astype(F32))
            if step == 5:
                finish(1, c, total + back_left[2, :, columns(c)].astype(F32))
            if step == 6:
                finish(0, c, total + back_left[1, :, columns(c)].astype(F32))
                returned[:, :, columns(c)] = grouped(
                    dot(pick_table, scaled[:, columns(c)])
                ).astype(BF16)
                to_all_experts(
                    lambda peer: rows_of(returned, c).at[peer],
                    rows_of(results, c),
                    out_send.at[c],
                    out_recv.at[c],
                )
                results[my_expert, :, columns(c)] = returned[my_expert, :, columns(c)]
    for c in every:
        wait_all(rows_of(results, c), experts_all - 1, out_recv.at[c])
        out[:, columns(c)] = dot(
            take_table[...], flat(results[:, :, columns(c)]).astype(BF16)
        ).astype(out.dtype)

    for sent in started:
        sent.wait_send()
    wait_all(counts_out, experts_all - 1, small_send.at[0])
    wait_all(totals_in, planes - 1, small_send.at[1])
    wait_all(gates_in, planes - 1, small_send.at[2])
    for c in every:
        wait_all(rows_of(packed, c), experts_all - 1, rows_send.at[c])
        wait_all(rows_of(returned, c), experts_all - 1, out_send.at[c])


def on_device(tokens, expert_ranks, capacity, weight_in, weight_out, gate_weights):
    planes = lax.axis_size("dp")
    experts_all = lax.axis_size("expert")
    token_count, width = tokens.shape
    block = gate_weights.shape[1]
    units = weight_in.shape[2]
    rows_all = experts_all * MOST
    chunks = len(SIXTEENTHS)
    anywhere = pl.BlockSpec(memory_space=pl.ANY)
    slots = pltpu.VMEM((6, block, width), BF16)
    exchange = pltpu.VMEM((experts_all, MOST, width), BF16)
    ring_sems = pltpu.SemaphoreType.DMA((2, 6, chunks))
    chunk_sems = pltpu.SemaphoreType.DMA((chunks,))
    return pl.pallas_call(
        layer_kernel,
        out_shape=pltpu.VMEM((token_count, width), BF16),
        in_specs=[pl.BlockSpec(memory_space=pltpu.SMEM)] + [anywhere] * 5,
        out_specs=pl.BlockSpec(memory_space=pltpu.VMEM),
        scratch_shapes=[
            pltpu.VMEM(tokens.shape, BF16),
            pltpu.VMEM(expert_ranks.shape, jnp.int32),
            pltpu.VMEM(gate_weights.shape, F32),
            pltpu.VMEM(weight_in.shape[1:], BF16),
            pltpu.VMEM(weight_out.shape[1:], BF16),
            pltpu.VMEM((5, block, width), BF16),
            slots, slots,
            pltpu.VMEM((8 * block, width), BF16),
            pltpu.VMEM((3 * block, units), BF16),
            pltpu.VMEM((8 * block, width), F32),
            slots, slots, slots, slots,
            pltpu.VMEM((5 * block, width), BF16),
            exchange, exchange, exchange, exchange,
            pltpu.VMEM((experts_all, 1, LANES), F32),
            pltpu.VMEM((experts_all, 1, LANES), F32),
            pltpu.VMEM((experts_all, LANES), F32),
            pltpu.VMEM((MOST, LANES), F32),
            pltpu.VMEM((planes, MOST, LANES), F32),
            pltpu.VMEM((MOST, block), F32),
            pltpu.VMEM((planes, MOST, block), F32),
            pltpu.VMEM((5 * block, LANES), F32),
            pltpu.VMEM((5 * block, rows_all), BF16),
            pltpu.VMEM((rows_all, LANES), F32),
            pltpu.VMEM((token_count, rows_all), BF16),
            pltpu.SemaphoreType.DMA((5,)),
            ring_sems, ring_sems, ring_sems, ring_sems,
            chunk_sems, chunk_sems, chunk_sems, chunk_sems,
            pltpu.SemaphoreType.DMA((3,)),
            pltpu.SemaphoreType.DMA((3,)),
        ],
        compiler_params=pltpu.CompilerParams(
            collective_id=0, has_side_effects=True, vmem_limit_bytes=57 * 1024 * 1024
        ),
        name="layer",
    )(capacity, tokens, expert_ranks, gate_weights, weight_in[0], weight_out[0])


def solution(mesh):
    both = ("dp", "expert")
    placed = (
        P(both, None),
        P(None, both),
        P(),
        P("expert", None, "dp"),
        P("expert", "dp", None),
        P("expert", "dp"),
    )
    return jax.shard_map(
        on_device, mesh=mesh, in_specs=placed, out_specs=P(both, None), check_vma=False
    )
```

time: 164 us -> 159 us (0.970)
  Pallas kernels: 162 us -> 158 us
    pallas_call x1, Pallas kernels: 162 us -> 158 us  [on_device(): pl.pallas_call(layer_kernel, out_shape=pltpu.VMEM((token_count, width), B...]
where the time goes in v3:
time: 159 us
  Pallas kernels  158 us (99%)
    pallas_call x1, Pallas kernels, on_device(): pl.pallas_call(layer_kernel, out_shape=pltpu.VMEM((token_count, width), B...  158 us

profile of v3, /device:TPU:1, one launch (start us, length us, event | category | flops | bytes accessed | tf_op | source)
XLA Modules:
  0.0 158.9 jit_solution(7348460589294160741)
XLA Ops:
  0.0 157.9 %layer.1 = bf16[256,2048]{1,0:T(8,128)(2,1)S(1)} custom-call(s32[32]{0:T(128)} %capacity.1, bf16[256,2048]{1,0:T(8,128)(2,1)} %tokens_hbm.1, s32[32,256]{1,0:T(8,128)} %ranks_hbm.1, f32[1,128]{1,0:T(1,128)} %gate_hbm.1, bf16[2048,1024]{1,0:T(8,128)(2,1)} %bitcast.2, bf16[1024,2048]{1,0:T(8,128)(2,1)} %bitcast.3), custom_call_target="tpu_custom_call" | custom-call | tf_op jit(solution)/shard_map/layer/pallas_call | solution.py:424
  157.9 1.0 copy.8

commit v4 on v3

--- a/solution.py
+++ b/solution.py
@@ -6,7 +6,7 @@
 from jax.sharding import PartitionSpec as P
 
 MOST = 8
-SIXTEENTHS = (4, 4, 4, 2, 2)
+SIXTEENTHS = (4, 4, 4, 4)
 FIRST_HALF = 2
 LANES = 128
 PLACE_IN_F = {2: 0, 1: 1, 3: 2, 0: 3, 4: 4, 5: 5, 7: 6, 6: 7}
@@ -28,8 +28,8 @@
 
 
 def layer_kernel(
-    capacity, tokens_hbm, ranks_hbm, gate_hbm, w_in_hbm, w_out_hbm, out,
-    tokens, ranks, gate_in, w_in, w_out, own, from_left, from_right, final, hidden, part,
+    capacity_hbm, tokens_hbm, ranks_hbm, gate_hbm, w_in_hbm, w_out_hbm, out,
+    capacity, tokens, ranks, gate_in, w_in, w_out, own, from_left, from_right, final, hidden, part,
     back_left, back_right, stage_right, stage_left, scaled,
     packed, arrived, returned, results, counts_out, counts_in, counts_flat, totals_out, totals_in,
     gates_out, gates_in, window_gate, place_table, target_column, take_table,
@@ -61,10 +61,11 @@
                 (tokens_hbm, tokens),
                 (w_in_hbm, w_in),
                 (w_out_hbm, w_out),
+                (capacity_hbm, capacity),
             )
         )
     ]
-    for load in loads[:3]:
+    for load in (loads[0], loads[5], loads[1], loads[2]):
         load.start()
 
     def partner(i):
@@ -72,12 +73,12 @@
 
     barrier = pltpu.get_barrier_semaphore()
 
-    @pl.loop(0, experts_all - 1)
+    @pl.loop(0, experts_all - 1, unroll=True)
     def _(i):
         peer = partner(i)
         pl.semaphore_signal(barrier, inc=1, device_id={"expert": peer}, device_id_type=MESH_ID)
 
-    @pl.loop(1, planes)
+    @pl.loop(1, planes, unroll=True)
     def _(i):
         peer = lax.rem(me + i, planes)
         pl.semaphore_signal(barrier, inc=1, device_id={"dp": peer}, device_id_type=MESH_ID)
@@ -124,6 +125,7 @@
     def rows_of(ref, c):
         return ref.at[:, :, columns(c)]
 
+    loads[5].wait()
     limits = jnp.zeros((experts_all, LANES), jnp.int32)
     for e in range(experts_all):
         limits = jnp.where(iota((experts_all, LANES), 0) == e, capacity[e], limits)
@@ -163,7 +165,7 @@
         arrived[my_expert, :, columns(c)] = packed[my_expert, :, columns(c)]
 
     loads[2].wait()
-    for load in loads[3:]:
+    for load in loads[3:5]:
         load.start()
     pack_rows(0)
     pack_rows(1)
@@ -186,6 +188,8 @@
     starts = dot(table_of(ahead), counts_table)
     place_in = (iota((rows_all, LANES), 0) % MOST).astype(F32)
     take_table[...] = pack.T.astype(BF16)
+    taken_row = jnp.where(place_in < counts, 1.0, 0.0).T[0:1, :] > 0.5
+    place_row = (starts + place_in).T[0:1, :]
     wait_all(totals_in, planes - 1, small_recv.at[1])
     plane_counts = [totals_in[z] for z in range(planes)]
     left_over = jnp.full((MOST, LANES), float(planes * block), F32)
@@ -204,10 +208,9 @@
         left_over = left_over - extra
         padded_start = padded_start + plane_counts[z] + extra
     base = drift_mine - drift_most + 4.0 * block
-    target = jnp.where(place_in < counts, base[0:1, :] + starts + place_in, -1.0)
-    target_column[...] = target
-    target_row = target.T[0:1, :]
+    target_row = jnp.where(taken_row, base[0:1, 0:1] + place_row, -1.0)
     place_table[...] = table_of(target_row == iota((window, rows_all), 0).astype(F32))
+    target_column[...] = jnp.where(place_in < counts, base[0:1, :] + starts + place_in, -1.0)
 
     def copy(src, dst, sends, recvs, way, step, c):
         return pltpu.make_async_remote_copy(
@@ -392,12 +395,6 @@
                     out_recv.at[c],
                 )
                 results[my_expert, :, columns(c)] = returned[my_expert, :, columns(c)]
-    for c in every:
-        wait_all(rows_of(results, c), experts_all - 1, out_recv.at[c])
-        out[:, columns(c)] = dot(
-            take_table[...], flat(results[:, :, columns(c)]).astype(BF16)
-        ).astype(out.dtype)
-
     for sent in started:
         sent.wait_send()
     wait_all(counts_out, experts_all - 1, small_send.at[0])
@@ -405,6 +402,13 @@
     wait_all(gates_in, planes - 1, small_send.at[2])
     for c in every:
         wait_all(rows_of(packed, c), experts_all - 1, rows_send.at[c])
+    for c in every:
+        wait_all(rows_of(results, c), experts_all - 1, out_recv.at[c])
+        out[:, columns(c)] = dot(
+            take_table[...], flat(results[:, :, columns(c)]).astype(BF16)
+        ).astype(out.dtype)
+
+    for c in every:
         wait_all(rows_of(returned, c), experts_all - 1, out_send.at[c])
 
 
@@ -424,9 +428,10 @@
     return pl.pallas_call(
         layer_kernel,
         out_shape=pltpu.VMEM((token_count, width), BF16),
-        in_specs=[pl.BlockSpec(memory_space=pltpu.SMEM)] + [anywhere] * 5,
+        in_specs=[anywhere] * 6,
         out_specs=pl.BlockSpec(memory_space=pltpu.VMEM),
         scratch_shapes=[
+            pltpu.SMEM(capacity.shape, jnp.int32),
             pltpu.VMEM(tokens.shape, BF16),
             pltpu.VMEM(expert_ranks.shape, jnp.int32),
             pltpu.VMEM(gate_weights.shape, F32),
@@ -451,7 +456,7 @@
             pltpu.VMEM((5 * block, rows_all), BF16),
             pltpu.VMEM((rows_all, LANES), F32),
             pltpu.VMEM((token_count, rows_all), BF16),
-            pltpu.SemaphoreType.DMA((5,)),
+            pltpu.SemaphoreType.DMA((6,)),
             ring_sems, ring_sems, ring_sems, ring_sems,
             chunk_sems, chunk_sems, chunk_sems, chunk_sems,
             pltpu.SemaphoreType.DMA((3,)),

time: 159 us -> 157 us (0.987)
  Pallas kernels: 158 us -> 156 us
where the time goes in v4:
time: 157 us
  Pallas kernels  156 us (99%)
    pallas_call x1, Pallas kernels, on_device(): pl.pallas_call(layer_kernel, out_shape=pltpu.VMEM((token_count, width), B...  156 us

profile of v4, /device:TPU:1, one launch (start us, length us, event | category | flops | bytes accessed | tf_op | source)
XLA Modules:
  0.0 157.3 jit_solution(12121829068315173485)
XLA Ops:
  0.0 156.4 %layer.1 = bf16[256,2048]{1,0:T(8,128)(2,1)S(1)} custom-call(s32[32]{0:T(128)} %capacity_hbm.1, bf16[256,2048]{1,0:T(8,128)(2,1)} %tokens_hbm.1, s32[32,256]{1,0:T(8,128)} %ranks_hbm.1, f32[1,128]{1,0:T(1,128)} %gate_hbm.1, bf16[2048,1024]{1,0:T(8,128)(2,1)} %bitcast.2, bf16[1024,2048]{1,0:T(8,128)(2,1)} %bitcast.3), custom_call_target="tpu_custom_call" | custom-call | tf_op jit(solution)/shard_map/layer/pallas_call | solution.py:428
  156.4 1.0 copy.8

commit v5 on v4

--- a/solution.py
+++ b/solution.py
@@ -32,7 +32,7 @@
     capacity, tokens, ranks, gate_in, w_in, w_out, own, from_left, from_right, final, hidden, part,
     back_left, back_right, stage_right, stage_left, scaled,
     packed, arrived, returned, results, counts_out, counts_in, counts_flat, totals_out, totals_in,
-    gates_out, gates_in, window_gate, place_table, target_column, take_table,
+    gates_out, gates_in, window_gate, place_table, target_column, take_table, first_rows,
     in_sem, send_sem, recv_sem, back_send_sem, back_recv_sem,
     rows_send, rows_recv, out_send, out_recv, small_send, small_recv,
 ):
@@ -137,13 +137,9 @@
     for e in range(experts_all):
         counts_out[e] = taken[e : e + 1, :]
     counts_in[my_expert] = counts_out[my_expert]
-    loads[1].wait()
-    gates_out[...] = jnp.broadcast_to(gate_in[...], gates_out.shape)
-    gates_in[me] = gates_out[...]
 
     pl.semaphore_wait(barrier, experts_all + planes - 2)
     to_all_experts(lambda peer: counts_out.at[peer], counts_in, small_send.at[0], small_recv.at[0])
-    to_all_planes(gates_out, gates_in, small_send.at[2], small_recv.at[2])
 
     earlier = table_of(iota((token_count, token_count), 0) < iota((token_count, token_count), 1))
     code = jnp.where(chosen, dot(chosen_table, earlier), -1.0).astype(BF16)
@@ -181,6 +177,10 @@
     totals_in[me] = totals_out[...]
     for c in every[2:]:
         pack_rows(c)
+    loads[1].wait()
+    gates_out[...] = jnp.broadcast_to(gate_in[...], gates_out.shape)
+    gates_in[me] = gates_out[...]
+    to_all_planes(gates_out, gates_in, small_send.at[2], small_recv.at[2])
     counts_table = counts.astype(BF16)
     row_ids = iota((rows_all, rows_all), 0)
     lane_ids = iota((rows_all, rows_all), 1)
@@ -190,6 +190,8 @@
     take_table[...] = pack.T.astype(BF16)
     taken_row = jnp.where(place_in < counts, 1.0, 0.0).T[0:1, :] > 0.5
     place_row = (starts + place_in).T[0:1, :]
+    wait_all(rows_of(arrived, 0), experts_all - 1, rows_recv.at[0])
+    first_rows[...] = flat(arrived[:, :, columns(0)]).astype(BF16)
     wait_all(totals_in, planes - 1, small_recv.at[1])
     plane_counts = [totals_in[z] for z in range(planes)]
     left_over = jnp.full((MOST, LANES), float(planes * block), F32)
@@ -255,8 +257,11 @@
         return flat(arrived[:, :, columns(c)]).astype(BF16)
 
     for c in every:
-        wait_all(rows_of(arrived, c), experts_all - 1, rows_recv.at[c])
-        rows = arrived_rows(c)
+        if c == 0:
+            rows = first_rows[...]
+        else:
+            wait_all(rows_of(arrived, c), experts_all - 1, rows_recv.at[c])
+            rows = arrived_rows(c)
         place(0, c, rows)
         send(own.at[0, :, columns(c)], 0, 1, c)
         place(4, c, rows)
@@ -456,6 +461,7 @@
             pltpu.VMEM((5 * block, rows_all), BF16),
             pltpu.VMEM((rows_all, LANES), F32),
             pltpu.VMEM((token_count, rows_all), BF16),
+            pltpu.VMEM((rows_all, width // 16 * SIXTEENTHS[0]), BF16),
             pltpu.SemaphoreType.DMA((6,)),
             ring_sems, ring_sems, ring_sems, ring_sems,
             chunk_sems, chunk_sems, chunk_sems, chunk_sems,

time: 157 us -> 158 us (level)
  no operation moved by 1% of the time
where the time goes in v5:
time: 158 us
  Pallas kernels  157 us (99%)
    pallas_call x1, Pallas kernels, on_device(): pl.pallas_call(layer_kernel, out_shape=pltpu.VMEM((token_count, width), B...  157 us

profile of v5, /device:TPU:1, one launch (start us, length us, event | category | flops | bytes accessed | tf_op | source)
XLA Modules:
  0.0 158.1 jit_solution(12445099497536625148)
XLA Ops:
  0.0 157.2 %layer.1 = bf16[256,2048]{1,0:T(8,128)(2,1)S(1)} custom-call(s32[32]{0:T(128)} %capacity_hbm.1, bf16[256,2048]{1,0:T(8,128)(2,1)} %tokens_hbm.1, s32[32,256]{1,0:T(8,128)} %ranks_hbm.1, f32[1,128]{1,0:T(1,128)} %gate_hbm.1, bf16[2048,1024]{1,0:T(8,128)(2,1)} %bitcast.2, bf16[1024,2048]{1,0:T(8,128)(2,1)} %bitcast.3), custom_call_target="tpu_custom_call" | custom-call | tf_op jit(solution)/shard_map/layer/pallas_call | solution.py:433
  157.2 1.0 copy.8
